TPU v7x, 32 devices: a whole 2x2x4 slice. The times are simulated.
32 devices in a mesh: rows: 8 (over y, x, core), model: 4 (over z).
Axes of the slice: x: 2, y: 2, z: 4, core: 2. Of those that a mesh axis runs over, the one named last changes fastest.
Arguments:
- one_query: float32 [5120, 5120], P('rows', 'model'), may hold values from -0.125 to 0.125
- other_query: float32 [5120, 5120], P('rows', 'model'), may hold values from -0.078125 to 0.078125
- one_key: float32 [5120, 5120], P('rows', 'model'), may hold values from -0.125 to 0.125
- other_key: float32 [5120, 5120], P('rows', 'model'), may hold values from -0.078125 to 0.078125
- one_value: float32 [5120, 5120], P('rows', 'model'), may hold values from -0.125 to 0.125
- other_value: float32 [5120, 5120], P('rows', 'model'), may hold values from -0.078125 to 0.078125
- mix_share: float32 [5120], P('rows'), may hold values from 0.2 to 0.8
- norm_gain: float32 [5120], P('rows'), may hold values from 0.25 to 1.75
Outputs:
- final_query: bfloat16 [5120, 5120], P(None, 'model')
- final_key: bfloat16 [5120, 5120], P(None, 'model')
- final_value: bfloat16 [5120, 5120], P(None, 'model')
- factor_query: float32 [5120], P('model')
- factor_key: float32 [5120], P('model')
- factor_value: float32 [5120], P('model')
All inputs are finite; a program needn't handle non-finite values. Where the computation divides by a largest or mean magnitude, that divisor is 1e-20 or more.
Results may differ from a plain program's by a relative error of at most 0.001.
Values may be sent and summed in bfloat16 or wider, within the bound.
A program may use at most 192 MiB of HBM per device.

v0:
```python
import jax
import jax.numpy as jnp
from jax import lax
from jax.sharding import PartitionSpec as P


def local(one_query, other_query, one_key, other_key, one_value, other_value, mix_share, norm_gain):
    result_query = mix_share[:, None] * one_query + (1.0 - mix_share[:, None]) * other_query
    result_key = mix_share[:, None] * one_key + (1.0 - mix_share[:, None]) * other_key
    result_value = mix_share[:, None] * one_value + (1.0 - mix_share[:, None]) * other_value
    result_gained_query = result_query * norm_gain[:, None]
    result_gained_key = result_key * norm_gain[:, None]
    result_gained_value = result_value * norm_gain[:, None]
    factor_query, factor_key, factor_value = lax.pmax(
        (
            jnp.max(jnp.abs(result_gained_query), axis=0),
            jnp.max(jnp.abs(result_gained_key), axis=0),
            jnp.max(jnp.abs(result_gained_value), axis=0),
        ),
        "rows",
    )
    narrow_query, narrow_key, narrow_value = (
        (result_gained_query / factor_query).astype(jnp.bfloat16),
        (result_gained_key / factor_key).astype(jnp.bfloat16),
        (result_gained_value / factor_value).astype(jnp.bfloat16),
    )
    final_query, final_key, final_value = (
        lax.all_gather(narrow_query, "rows", axis=0, tiled=True),
        lax.all_gather(narrow_key, "rows", axis=0, tiled=True),
        lax.all_gather(narrow_value, "rows", axis=0, tiled=True),
    )
    return (final_query, final_key, final_value, factor_query, factor_key, factor_value)


def solution(mesh):
    placed = (
        P("rows", "model"),
        P("rows", "model"),
        P("rows", "model"),
        P("rows", "model"),
        P("rows", "model"),
        P("rows", "model"),
        P("rows"),
        P("rows"),
    )
    return jax.shard_map(
        local,
        mesh=mesh,
        in_specs=placed,
        out_specs=(
            P(None, "model"),
            P(None, "model"),
            P(None, "model"),
            P("model"),
            P("model"),
            P("model"),
        ),
        check_vma=False,
    )
```

profile of v0, /device:TPU:0, one launch (start us, length us, event | category | flops | bytes accessed | tf_op | source)
XLA Modules:
  0.0 307.9 jit_solution(9677748972599385960)
XLA Ops:
  7.2 0.0 all-gather.4.cloned.1.call-start
  7.2 0.7 broadcast_subtract_fusion
  7.9 10.6 %abs_reduce_fusion = (f32[1280]{0:T(1024)S(1)}, f32[640,1280]{1,0:T(8,128)S(1)}, f32[1280]{0:T(1024)S(1)}, f32[640,1280]{1,0:T(8,128)}, f32[1280]{0:T(1024)S(1)}, /*index=5*/f32[640,1280]{1,0:T(8,128)}) fusion(f32[640]{0:T(1024)} %param.15, f32[640,1280]{1,0:T(8,128)} %param.13, f32[640]{0:T(1024)S(1)} %broadcast_subtract_fusion, f32[640,1280]{1,0:T(8,128)} %param.12, ...), kind=kLoop, calls=%fused_computation.1 | loop fusion | flops 14741760 | bytes 29514240 | tf_op jit(solution)/shard_map/reduce_max | solution.py:18
  18.5 25.5 %all-reduce = (f32[1280]{0:T(1024)S(1)}, f32[1280]{0:T(1024)S(1)}, f32[1280]{0:T(1024)S(1)}) all-reduce(f32[1280]{0:T(1024)S(1)} %get-tuple-element.17, f32[1280]{0:T(1024)S(1)} %get-tuple-element.15, f32[1280]{0:T(1024)S(1)} %get-tuple-element.9), channel_id=1, replica_groups=mesh['rows'=8,'model'=4] {'rows'}, use_global_device_ids=true, to_apply=%region_1.0 | all-reduce | flops 3840 | bytes 30720 | tf_op jit(solution)/shard_map/pmax | solution.py:14
  44.0 0.0 copy-start.3
  44.0 3.3 %divide_convert_fusion.2 = bf16[640,1280]{1,0:T(8,128)(2,1)} fusion(f32[640,1280]{1,0:T(8,128)} %get-tuple-element.18, f32[1280]{0:T(1024)S(1)} %get-tuple-element.28), kind=kLoop, calls=%fused_computation.6 | loop fusion | flops 1638400 | bytes 4920320 | tf_op jit(solution)/shard_map/convert_element_type | solution.py:23
  47.4 0.0 all-gather.4.cloned.1.call-update
  47.4 0.0 all-gather.6.cloned.1.call-start
  47.5 3.3 %divide_convert_fusion.1 = bf16[640,1280]{1,0:T(8,128)(2,1)} fusion(f32[640,1280]{1,0:T(8,128)} %get-tuple-element.16, f32[1280]{0:T(1024)S(1)} %get-tuple-element.29), kind=kLoop, calls=%fused_computation.3 | loop fusion | flops 1638400 | bytes 4920320 | tf_op jit(solution)/shard_map/convert_element_type | solution.py:24
  50.8 0.0 all-gather.6.cloned.1.call-update
  50.8 0.0 all-gather.8.cloned.1.call-start
  50.9 0.0 copy-done.3
  50.9 1.4 divide_convert_fusion
  52.3 0.0 all-gather.8.cloned.1.call-update
  52.3 68.8 %all-gather.4.cloned.1.call-done = bf16[5120,1280]{1,0:T(8,128)(2,1)} async-done(((bf16[640,1280]{1,0:T(8,128)(2,1)}), bf16[5120,1280]{1,0:T(8,128)(2,1)}) %all-gather.4.cloned.1.call-update) | async-done | bytes 13107216 | tf_op jit(solution)/shard_map/all_gather | solution.py:28
  121.1 76.7 %all-gather.6.cloned.1.call-done = bf16[5120,1280]{1,0:T(8,128)(2,1)} async-done(((bf16[640,1280]{1,0:T(8,128)(2,1)}), bf16[5120,1280]{1,0:T(8,128)(2,1)}) %all-gather.6.cloned.1.call-update) | async-done | bytes 13107216 | tf_op jit(solution)/shard_map/all_gather | solution.py:29
  197.8 76.7 %all-gather.8.cloned.1.call-done = bf16[5120,1280]{1,0:T(8,128)(2,1)} async-done(((bf16[640,1280]{1,0:T(8,128)(2,1)}), bf16[5120,1280]{1,0:T(8,128)(2,1)}) %all-gather.8.cloned.1.call-update) | async-done | bytes 13107216 | tf_op jit(solution)/shard_map/all_gather | solution.py:30
  274.6 12.6 %copy.17 = bf16[5120,1280]{1,0:T(8,128)(2,1)} copy(bf16[5120,1280]{1,0:T(8,128)(2,1)} %all-gather.4.cloned.1.call-done) | data formatting | bytes 26214400
  287.2 0.1 copy-done
  287.3 6.6 %copy.18 = bf16[5120,1280]{1,0:T(8,128)(2,1)} copy(bf16[5120,1280]{1,0:T(8,128)(2,1)S(1)} %copy-done) | data formatting | bytes 26214400
  294.0 1.1 slice-done.1
  295.1 1.2 slice-done.2
  296.3 0.1 slice-done.3
  296.4 4.9 %copy.19 = bf16[5120,1280]{1,0:T(8,128)(2,1)} copy(bf16[5120,1280]{1,0:T(8,128)(2,1)S(1)} %bitcast.1) | data formatting | bytes 26214400
  (11 shorter events, 0.0 us)
Async XLA Ops:
  7.2 114.0 %all-gather.4.cloned.1.call-start = ((), (), s32[]{:S(2)}) async-start(), calls=%async_computation | async-start | bytes 14745600 | tf_op jit(solution)/shard_map/all_gather | solution.py:28
  44.0 3.4 %copy-start.1 = (f32[1280]{0:T(1024)}, f32[1280]{0:T(1024)S(1)}, u32[]{:S(2)}) copy-start(f32[1280]{0:T(1024)S(1)} %get-tuple-element.28) | copy-start | bytes 15364
  44.0 3.4 %copy-start.2 = (f32[1280]{0:T(1024)}, f32[1280]{0:T(1024)S(1)}, u32[]{:S(2)}) copy-start(f32[1280]{0:T(1024)S(1)} %get-tuple-element.29) | copy-start | bytes 15364
  44.0 6.8 %copy-start.3 = (f32[1280]{0:T(1024)}, f32[1280]{0:T(1024)S(1)}, u32[]{:S(2)}) copy-start(f32[1280]{0:T(1024)S(1)} %get-tuple-element.30) | copy-start | bytes 15364
  47.4 150.4 %all-gather.6.cloned.1.call-start = ((), (), s32[]{:S(2)}) async-start(), calls=%async_computation.1 | async-start | bytes 14745600 | tf_op jit(solution)/shard_map/all_gather | solution.py:29
  50.8 223.7 %all-gather.8.cloned.1.call-start = ((), (), s32[]{:S(2)}) async-start(), calls=%async_computation.2 | async-start | bytes 14745600 | tf_op jit(solution)/shard_map/all_gather | solution.py:30
  274.6 12.8 %copy-start = (bf16[5120,1280]{1,0:T(8,128)(2,1)S(1)}, bf16[5120,1280]{1,0:T(8,128)(2,1)}, u32[]{:S(2)}) copy-start(bf16[5120,1280]{1,0:T(8,128)(2,1)} %all-gather.6.cloned.1.call-done) | copy-start | bytes 39321604
  274.6 19.4 %slice-start = ((s8[13107200]{0:T(1024)(128)(4,1)}), s8[4194304]{0:T(1024)(128)(4,1)S(1)}, s32[]{:S(2)}) async-start(s8[13107200]{0:T(1024)(128)(4,1)} %bitcast), calls=%async_computation.3 | async-start | bytes 8388608
  274.6 20.5 %slice-start.1 = ((s8[13107200]{0:T(1024)(128)(4,1)}), s8[4194304]{0:T(1024)(128)(4,1)S(1)}, s32[]{:S(2)}) async-start(s8[13107200]{0:T(1024)(128)(4,1)} %bitcast), calls=%async_computation.4 | async-start | bytes 8388608
  274.6 21.7 %slice-start.2 = ((s8[13107200]{0:T(1024)(128)(4,1)}), s8[4194304]{0:T(1024)(128)(4,1)S(1)}, s32[]{:S(2)}) async-start(s8[13107200]{0:T(1024)(128)(4,1)} %bitcast), calls=%async_computation.5 | async-start | bytes 8388608
  287.3 9.0 %slice-start.3 = ((s8[13107200]{0:T(1024)(128)(4,1)}), s8[524288]{0:T(1024)(128)(4,1)S(1)}, s32[]{:S(2)}) async-start(s8[13107200]{0:T(1024)(128)(4,1)} %bitcast), calls=%async_computation.6 | async-start | bytes 1048576
Sparse Core Ops, SparseCore 0:
  47.5 73.5 all-gather.3
  123.6 74.1 all-gather.5
  200.3 74.1 all-gather.7
where the time goes:
time: 308 us
  waiting for transfers between devices  222 us (72%)
  local copies, waits for them, and re-layouts  26.8 us (9%)
  blocking collectives  25.5 us (8%)
  other arithmetic  19.4 us (6%)
  between operations  13.8 us (4%)
    all_gather x1, waiting for transfers between devices, local(): lax.all_gather(narrow_value, 'rows', axis=0, tiled=True)  76.7 us
    all_gather x1, waiting for transfers between devices, local(): lax.all_gather(narrow_key, 'rows', axis=0, tiled=True)  76.7 us
    all_gather x1, waiting for transfers between devices, local(): lax.all_gather(narrow_query, 'rows', axis=0, tiled=True)  68.8 us
    unnamed x19, local copies, waits for them, and re-layouts  26.8 us
    pmax x1, blocking collectives, local(): lax.pmax((jnp.max(jnp.abs(result_gained_query), axis=0), jnp.max(jnp.abs(...  25.5 us
    reduce_max x1, other arithmetic, local(): jnp.max(jnp.abs(result_gained_value), axis=0)  10.6 us
  transfers between devices with their start and end apart: 3, of which 3 were waited for; matrix products, arithmetic and copies ran while one was open for 2% of the time, Pallas kernels for 0%

commit v1 on v0

v1 whole, which is shorter than its diff:
```python
import functools

import jax
import jax.numpy as jnp
from jax import lax
from jax.experimental import pallas as pl
from jax.experimental.pallas import tpu as pltpu
from jax.sharding import PartitionSpec as P

MESH = pl.DeviceIdType.MESH
LANES = 128
IN_VMEM = 0
OWN_X, OWN_Y, OWN_S, DIAG, X_S, Y_S, D_S = range(7)


def gathered_by_collectives(one_query, other_query, one_key, other_key, one_value, other_value, mix_share, norm_gain):
    share, gain = mix_share[:, None], norm_gain[:, None]
    gained = [
        (share * one + (1.0 - share) * other) * gain
        for one, other in ((one_query, other_query), (one_key, other_key), (one_value, other_value))
    ]
    factors = lax.pmax(tuple(jnp.max(jnp.abs(g), axis=0) for g in gained), "rows")
    narrow = [(g / f).astype(jnp.bfloat16) for g, f in zip(gained, factors)]
    return (*(lax.all_gather(w, "rows", axis=0, tiled=True) for w in narrow), *factors)


def kernel(chunks, share, gain, *refs):
    args, outs, factors = refs[0:6], refs[6:9], refs[9:12]
    (held, wide_one, wide_other, box_first, box_rest, staged,
     load_sem, send_sem, bulk_sem, x_sem, y_sem, d_sem, box_sem, keep_sem) = refs[12:]
    rows, columns = args[0].shape
    height = rows // chunks
    half = chunks // 2
    tiles = columns // LANES

    me = lax.axis_index("rows")
    core, east, north = lax.rem(me, 2), lax.rem(me // 2, 2), me // 4

    def peer(d):
        return (
            lax.rem(north + d // 4, 2) * 4
            + lax.rem(east + (d // 2) % 2, 2) * 2
            + lax.rem(core + d % 2, 2)
        )

    sibling, at_x, at_y, at_d = peer(1), peer(2), peer(4), peer(6)

    loads = [pltpu.make_async_copy(args[i], held.at[i], load_sem.at[i]) for i in range(6)]
    for load in loads:
        load.start()

    barrier = pltpu.get_barrier_semaphore()
    for d in range(1, 8):
        pl.semaphore_signal(barrier, inc=1, device_id={"rows": peer(d)}, device_id_type=MESH)

    for j in range(rows // LANES):
        s = jnp.broadcast_to(share[:, j * LANES:(j + 1) * LANES], (LANES, LANES)).T
        g = jnp.broadcast_to(gain[:, j * LANES:(j + 1) * LANES], (LANES, LANES)).T
        wide_one[j * LANES:(j + 1) * LANES, :] = s * g
        wide_other[j * LANES:(j + 1) * LANES, :] = (1.0 - s) * g

    def mix(m):
        loads[2 * m].wait()
        loads[2 * m + 1].wait()

        def body(i, top):
            at = pl.ds(pl.multiple_of(i * 8, 8), 8)
            a = jnp.concatenate([wide_one[at, :]] * tiles, axis=1)
            b = jnp.concatenate([wide_other[at, :]] * tiles, axis=1)
            mixed = a * held[2 * m, at, :] + b * held[2 * m + 1, at, :]
            held[2 * m, at, :] = mixed
            return jnp.maximum(top, jnp.abs(mixed))

        top = lax.fori_loop(0, rows // 8, body, jnp.zeros((8, columns), jnp.float32), unroll=4)
        return jnp.max(top, axis=0, keepdims=True)

    def exchange(box, which):
        return [
            pltpu.make_async_remote_copy(
                box.at[me], box.at[me], box_sem.at[2 * which], box_sem.at[2 * which + 1],
                device_id={"rows": peer(d)}, device_id_type=MESH,
            )
            for d in range(1, 8)
        ]

    def exchanged(box, which):
        return pltpu.make_async_remote_copy(
            box.at[pl.ds(0, 7)], box.at[pl.ds(0, 7)], box_sem.at[2 * which], box_sem.at[2 * which + 1],
            device_id={"rows": sibling}, device_id_type=MESH,
        )

    def piece(m, owner, k):
        return outs[m].at[pl.ds(pl.multiple_of(owner * rows + k * height, 16), height), :]

    def copy(m, owner, k, stream, target):
        ref = piece(m, owner, k)
        source = ref
        if m >= IN_VMEM and stream in (OWN_X, OWN_Y, OWN_S):
            source = staged.at[m - IN_VMEM, pl.ds(k * height, height), :]
        arrive = {OWN_X: x_sem, OWN_Y: y_sem, DIAG: d_sem}.get(stream)
        arrive = bulk_sem.at[m, stream] if arrive is None else arrive.at[m, k]
        return pltpu.make_async_remote_copy(
            source, ref, send_sem.at[m, stream], arrive,
            device_id={"rows": target}, device_id_type=MESH,
        )

    def whole(m, stream):
        ref = outs[m].at[pl.ds(0, rows), :]
        return pltpu.make_async_remote_copy(
            ref, ref, send_sem.at[m, stream], bulk_sem.at[m, stream],
            device_id={"rows": sibling}, device_id_type=MESH,
        )

    def narrow(m, k, inverse):
        def body(i, _):
            at = pl.multiple_of(k * height + i * 16, 16)
            small = (held[2 * m, pl.ds(at, 16), :] * inverse).astype(jnp.bfloat16)
            if m < IN_VMEM:
                outs[m][pl.ds(pl.multiple_of(me * rows + at, 16), 16), :] = small
            else:
                staged[m - IN_VMEM, pl.ds(at, 16), :] = small
            return 0

        lax.fori_loop(0, height // 16, body, 0, unroll=True)

    def send_own(m, k):
        copy(m, me, k, OWN_X, at_x).start()
        copy(m, me, k, OWN_Y, at_y).start()
        copy(m, me, k, OWN_S, sibling).start()

    box_first[me] = mix(0)
    pl.semaphore_wait(barrier, 7)
    for c in exchange(box_first, 0):
        c.start()
    exchanged(box_first, 0).wait_recv()
    factor = jnp.max(box_first[...], axis=0)
    factors[0][...] = factor
    inverse = 1.0 / factor
    for k in range(chunks):
        narrow(0, k, inverse)
        if 1 <= k <= half:
            send_own(0, k - 1)

    box_rest[me, 0:1] = mix(1)
    box_rest[me, 1:2] = mix(2)
    for c in exchange(box_rest, 1):
        c.start()
    for k in range(half, chunks):
        send_own(0, k)
    exchanged(box_rest, 1).wait_recv()
    both = jnp.max(box_rest[...], axis=0)
    for m in (1, 2):
        factor = both[m - 1:m]
        factors[m][...] = factor
        inverse = 1.0 / factor
        for k in range(chunks):
            narrow(m, k, inverse)
            if k:
                send_own(m, k - 1)
        send_own(m, chunks - 1)
    kept = [
        pltpu.make_async_copy(
            staged.at[m - IN_VMEM],
            outs[m].at[pl.ds(pl.multiple_of(me * rows, 16), rows), :],
            keep_sem.at[m],
        )
        for m in range(IN_VMEM, 3)
    ]
    for keep in kept:
        keep.start()

    for m in range(3):
        for k in range(chunks):
            copy(m, at_x, k, OWN_X, at_x).wait_recv()
            copy(m, at_x, k, X_S, sibling).start()
            if k < half:
                copy(m, at_x, k, DIAG, at_y).start()
            copy(m, at_y, k, OWN_Y, at_y).wait_recv()
            copy(m, at_y, k, Y_S, sibling).start()
            if k >= half:
                copy(m, at_y, k, DIAG, at_x).start()
    for m in range(3):
        for k in range(half):
            for part in (k, k + half):
                copy(m, at_d, part, DIAG, at_y).wait_recv()
                copy(m, at_d, part, D_S, sibling).start()

    for m in range(3):
        for stream in (OWN_S, X_S, Y_S, D_S):
            whole(m, stream).wait_recv()
    for m in range(3):
        for stream in range(7):
            whole(m, stream).wait_send()
    for keep in kept:
        keep.wait()
    exchanged(box_first, 0).wait_send()
    exchanged(box_rest, 1).wait_send()


def gathered_by_kernel(*arrays):
    *weights, mix_share, norm_gain = arrays
    rows, columns = weights[0].shape
    chunks = 8
    vmem, hbm = pl.BlockSpec(memory_space=pltpu.VMEM), pl.BlockSpec(memory_space=pltpu.HBM)
    dma = pltpu.SemaphoreType.DMA
    results = pl.pallas_call(
        functools.partial(kernel, chunks),
        out_shape=[pltpu.VMEM((8 * rows, columns), jnp.bfloat16)] * IN_VMEM
        + [jax.ShapeDtypeStruct((8 * rows, columns), jnp.bfloat16)] * (3 - IN_VMEM)
        + [jax.ShapeDtypeStruct((1, columns), jnp.float32)] * 3,
        in_specs=[vmem] * 2 + [hbm] * 6,
        out_specs=[vmem] * IN_VMEM + [hbm] * (3 - IN_VMEM) + [vmem] * 3,
        scratch_shapes=[
            pltpu.VMEM((6, rows, columns), jnp.float32),
            pltpu.VMEM((rows, LANES), jnp.float32),
            pltpu.VMEM((rows, LANES), jnp.float32),
            pltpu.VMEM((8, 1, columns), jnp.float32),
            pltpu.VMEM((8, 2, columns), jnp.float32),
            pltpu.VMEM((max(3 - IN_VMEM, 1), rows, columns), jnp.bfloat16),
            dma((6,)),
            dma((3, 7)),
            dma((3, 7)),
            dma((3, chunks)),
            dma((3, chunks)),
            dma((3, chunks)),
            dma((4,)),
            dma((3,)),
        ],
        compiler_params=pltpu.CompilerParams(
            collective_id=0, has_side_effects=True, vmem_limit_bytes=26 * 2**20
        ),
    )(mix_share[None], norm_gain[None], *weights)
    return (*results[:3], *(f[0] for f in results[3:]))


def solution(mesh):
    placed = (P("rows", "model"),) * 6 + (P("rows"),) * 2
    local = gathered_by_kernel if mesh.shape["rows"] == 8 else gathered_by_collectives
    return jax.shard_map(
        local,
        mesh=mesh,
        in_specs=placed,
        out_specs=(P(None, "model"),) * 3 + (P("model"),) * 3,
        check_vma=False,
    )
```

time: 308 us -> 215 us (0.70)
  waiting for transfers between devices: 222 us -> 0 us
  Pallas kernels: 0 us -> 173 us
  blocking collectives: 25.5 us -> 0 us
  other arithmetic: 19.4 us -> 1.85 us
  between operations: 13.8 us -> 0.66 us
  local copies, waits for them, and re-layouts: 26.8 us -> 39.7 us
    all_gather x3 -> x0, waiting for transfers between devices: 222 us -> none  [the longest x1 76.7 us: local(): lax.all_gather(narrow_value, 'rows', axis=0, tiled=True)]
    pallas_call x0 -> x1, Pallas kernels: none -> 173 us  [gathered_by_kernel(): pl.pallas_call(functools.partial(kernel, chunks), out_shape=[pltpu.VMEM((...]
    pmax x1 -> x0, blocking collectives: 25.5 us -> none  [local(): lax.pmax((jnp.max(jnp.abs(result_gained_query), axis=0), jnp.max(jnp.abs(...]
    unnamed x19 -> x25, local copies, waits for them, and re-layouts: 26.8 us -> 38.3 us
    reduce_max x1 -> x0, other arithmetic: 10.6 us -> none  [local(): jnp.max(jnp.abs(result_gained_value), axis=0)]
    convert_element_type x3 -> x0, other arithmetic: 8.07 us -> none  [the longest x1 3.33 us: local(): (result_gained_query / factor_query).astype(jnp.bfloat16)]
  transfers between devices with their start and end apart: 3 -> 0, of which waited for: 3 -> 0; matrix products, arithmetic and copies ran while one was open for 2% -> 0% of each run, Pallas kernels for 0% -> 0%
where the time goes in v1:
time: 215 us
  Pallas kernels  173 us (80%)
  local copies, waits for them, and re-layouts  39.7 us (18%)
    pallas_call x1, Pallas kernels, gathered_by_kernel(): pl.pallas_call(functools.partial(kernel, chunks), out_shape=[pltpu.VMEM((...  173 us
    unnamed x25, local copies, waits for them, and re-layouts  38.3 us

profile of v1, /device:TPU:0, one launch (start us, length us, event | category | flops | bytes accessed | tf_op | source)
XLA Modules:
  0.0 215.0 jit_solution(9947456329554534991)
XLA Ops:
  0.6 0.7 broadcast_in_dim.6.share
  1.3 0.7 broadcast_in_dim.7.gain
  2.0 0.0 copy-start
  2.0 1.9 copy-done
  3.9 0.0 copy-start.1
  3.9 1.9 copy-done.1
  5.9 0.0 copy-start.2
  5.9 1.9 copy-done.2
  7.8 0.0 copy-start.3
  7.8 1.9 copy-done.3
  9.7 1.9 copy-done.4
  11.6 1.9 copy-done.5
  13.6 172.8 %shard_map.127 = (bf16[5120,1280]{1,0:T(8,128)(2,1)}, bf16[5120,1280]{1,0:T(8,128)(2,1)}, bf16[5120,1280]{1,0:T(8,128)(2,1)}, f32[1,1280]{1,0:T(1,128)S(1)}, f32...) custom-call(f32[1,640]{1,0:T(1,128)S(1)} %broadcast_in_dim.6.share, f32[1,640]{1,0:T(1,128)S(1)} %broadcast_in_dim.7.gain, ...), custom_call_target="tpu_custom_call" | custom-call | tf_op jit(solution)/shard_map/pallas_call | solution.py:206
  186.4 0.6 reduce
  187.0 0.6 reduce.1
  187.7 0.6 reduce.2
  188.3 12.6 %copy.17 = bf16[5120,1280]{1,0:T(8,128)(2,1)} copy(bf16[5120,1280]{1,0:T(8,128)(2,1)} %get-tuple-element.24) | data formatting | bytes 26214400
  200.9 0.1 copy-done.6
  201.1 6.6 %copy.18 = bf16[5120,1280]{1,0:T(8,128)(2,1)} copy(bf16[5120,1280]{1,0:T(8,128)(2,1)S(1)} %copy-done.6) | data formatting | bytes 26214400
  207.7 0.0 slice-done
  207.7 1.1 slice-done.1
  208.8 1.3 slice-done.2
  210.1 0.0 slice-done.3
  210.1 4.9 %copy.19 = bf16[5120,1280]{1,0:T(8,128)(2,1)} copy(bf16[5120,1280]{1,0:T(8,128)(2,1)S(1)} %bitcast.1) | data formatting | bytes 26214400
  (8 shorter events, 0.0 us)
Async XLA Ops:
  2.0 1.9 copy-start
  3.9 1.9 copy-start.1
  5.9 1.9 copy-start.2
  7.8 1.9 copy-start.3
  9.7 1.9 copy-start.4
  11.6 1.9 copy-start.5
  188.3 12.8 %copy-start.6 = (bf16[5120,1280]{1,0:T(8,128)(2,1)S(1)}, bf16[5120,1280]{1,0:T(8,128)(2,1)}, u32[]{:S(2)}) copy-start(bf16[5120,1280]{1,0:T(8,128)(2,1)} %get-tuple-element.25) | copy-start | bytes 39321604
  188.3 19.4 %slice-start = ((s8[13107200]{0:T(1024)(128)(4,1)}), s8[4194304]{0:T(1024)(128)(4,1)S(1)}, s32[]{:S(2)}) async-start(s8[13107200]{0:T(1024)(128)(4,1)} %bitcast), calls=%async_computation | async-start | bytes 8388608
  188.3 20.5 %slice-start.1 = ((s8[13107200]{0:T(1024)(128)(4,1)}), s8[4194304]{0:T(1024)(128)(4,1)S(1)}, s32[]{:S(2)}) async-start(s8[13107200]{0:T(1024)(128)(4,1)} %bitcast), calls=%async_computation.1 | async-start | bytes 8388608
  201.0 9.0 %slice-start.2 = ((s8[13107200]{0:T(1024)(128)(4,1)}), s8[4194304]{0:T(1024)(128)(4,1)S(1)}, s32[]{:S(2)}) async-start(s8[13107200]{0:T(1024)(128)(4,1)} %bitcast), calls=%async_computation.2 | async-start | bytes 8388608
  201.1 9.0 %slice-start.3 = ((s8[13107200]{0:T(1024)(128)(4,1)}), s8[524288]{0:T(1024)(128)(4,1)S(1)}, s32[]{:S(2)}) async-start(s8[13107200]{0:T(1024)(128)(4,1)} %bitcast), calls=%async_computation.3 | async-start | bytes 1048576

commit v2 on v1

--- a/solution.py
+++ b/solution.py
@@ -9,7 +9,6 @@
 
 MESH = pl.DeviceIdType.MESH
 LANES = 128
-IN_VMEM = 0
 OWN_X, OWN_Y, OWN_S, DIAG, X_S, Y_S, D_S = range(7)
 
 
@@ -25,9 +24,10 @@
 
 
 def kernel(chunks, share, gain, *refs):
-    args, outs, factors = refs[0:6], refs[6:9], refs[9:12]
-    (held, wide_one, wide_other, box_first, box_rest, staged,
-     load_sem, send_sem, bulk_sem, x_sem, y_sem, d_sem, box_sem, keep_sem) = refs[12:]
+    args, factors = refs[0:6], refs[6]
+    outs = [refs[7].at[m] for m in range(3)]
+    (held, wide_one, wide_other, box_first, box_rest,
+     load_sem, send_sem, bulk_sem, x_sem, y_sem, d_sem, box_sem) = refs[8:]
     rows, columns = args[0].shape
     height = rows // chunks
     half = chunks // 2
@@ -94,13 +94,10 @@
 
     def copy(m, owner, k, stream, target):
         ref = piece(m, owner, k)
-        source = ref
-        if m >= IN_VMEM and stream in (OWN_X, OWN_Y, OWN_S):
-            source = staged.at[m - IN_VMEM, pl.ds(k * height, height), :]
         arrive = {OWN_X: x_sem, OWN_Y: y_sem, DIAG: d_sem}.get(stream)
         arrive = bulk_sem.at[m, stream] if arrive is None else arrive.at[m, k]
         return pltpu.make_async_remote_copy(
-            source, ref, send_sem.at[m, stream], arrive,
+            ref, ref, send_sem.at[m, stream], arrive,
             device_id={"rows": target}, device_id_type=MESH,
         )
 
@@ -115,10 +112,7 @@
         def body(i, _):
             at = pl.multiple_of(k * height + i * 16, 16)
             small = (held[2 * m, pl.ds(at, 16), :] * inverse).astype(jnp.bfloat16)
-            if m < IN_VMEM:
-                outs[m][pl.ds(pl.multiple_of(me * rows + at, 16), 16), :] = small
-            else:
-                staged[m - IN_VMEM, pl.ds(at, 16), :] = small
+            outs[m][pl.ds(pl.multiple_of(me * rows + at, 16), 16), :] = small
             return 0
 
         lax.fori_loop(0, height // 16, body, 0, unroll=True)
@@ -134,7 +128,7 @@
         c.start()
     exchanged(box_first, 0).wait_recv()
     factor = jnp.max(box_first[...], axis=0)
-    factors[0][...] = factor
+    factors[0] = factor
     inverse = 1.0 / factor
     for k in range(chunks):
         narrow(0, k, inverse)
@@ -151,23 +145,13 @@
     both = jnp.max(box_rest[...], axis=0)
     for m in (1, 2):
         factor = both[m - 1:m]
-        factors[m][...] = factor
+        factors[m] = factor
         inverse = 1.0 / factor
         for k in range(chunks):
             narrow(m, k, inverse)
             if k:
                 send_own(m, k - 1)
         send_own(m, chunks - 1)
-    kept = [
-        pltpu.make_async_copy(
-            staged.at[m - IN_VMEM],
-            outs[m].at[pl.ds(pl.multiple_of(me * rows, 16), rows), :],
-            keep_sem.at[m],
-        )
-        for m in range(IN_VMEM, 3)
-    ]
-    for keep in kept:
-        keep.start()
 
     for m in range(3):
         for k in range(chunks):
@@ -191,10 +175,19 @@
     for m in range(3):
         for stream in range(7):
             whole(m, stream).wait_send()
-    for keep in kept:
-        keep.wait()
     exchanged(box_first, 0).wait_send()
     exchanged(box_rest, 1).wait_send()
+
+
+def settle(factors, gathered, *refs):
+    targets, sems = refs[:6], refs[6]
+    copies = [pltpu.make_async_copy(gathered.at[m], targets[m], sems.at[m]) for m in range(3)]
+    for c in copies:
+        c.start()
+    for m in range(3):
+        targets[3 + m][...] = factors[m, 0]
+    for c in copies:
+        c.wait()
 
 
 def gathered_by_kernel(*arrays):
@@ -205,18 +198,18 @@
     dma = pltpu.SemaphoreType.DMA
     results = pl.pallas_call(
         functools.partial(kernel, chunks),
-        out_shape=[pltpu.VMEM((8 * rows, columns), jnp.bfloat16)] * IN_VMEM
-        + [jax.ShapeDtypeStruct((8 * rows, columns), jnp.bfloat16)] * (3 - IN_VMEM)
-        + [jax.ShapeDtypeStruct((1, columns), jnp.float32)] * 3,
+        out_shape=[
+            pltpu.VMEM((3, 1, columns), jnp.float32),
+            pltpu.VMEM((3, 8 * rows, columns), jnp.bfloat16),
+        ],
         in_specs=[vmem] * 2 + [hbm] * 6,
-        out_specs=[vmem] * IN_VMEM + [hbm] * (3 - IN_VMEM) + [vmem] * 3,
+        out_specs=[vmem] * 2,
         scratch_shapes=[
             pltpu.VMEM((6, rows, columns), jnp.float32),
             pltpu.VMEM((rows, LANES), jnp.float32),
             pltpu.VMEM((rows, LANES), jnp.float32),
             pltpu.VMEM((8, 1, columns), jnp.float32),
             pltpu.VMEM((8, 2, columns), jnp.float32),
-            pltpu.VMEM((max(3 - IN_VMEM, 1), rows, columns), jnp.bfloat16),
             dma((6,)),
             dma((3, 7)),
             dma((3, 7)),
@@ -224,13 +217,23 @@
             dma((3, chunks)),
             dma((3, chunks)),
             dma((4,)),
-            dma((3,)),
         ],
         compiler_params=pltpu.CompilerParams(
-            collective_id=0, has_side_effects=True, vmem_limit_bytes=26 * 2**20
+            collective_id=0, has_side_effects=True, vmem_limit_bytes=22 * 2**20
         ),
     )(mix_share[None], norm_gain[None], *weights)
-    return (*results[:3], *(f[0] for f in results[3:]))
+    results = [pltpu.with_memory_space_constraint(r, pltpu.VMEM) for r in results]
+    return tuple(
+        pl.pallas_call(
+            settle,
+            out_shape=[jax.ShapeDtypeStruct((8 * rows, columns), jnp.bfloat16)] * 3
+            + [jax.ShapeDtypeStruct((columns,), jnp.float32)] * 3,
+            in_specs=[vmem] * 2,
+            out_specs=[pl.BlockSpec(memory_space=pl.ANY)] * 3 + [vmem] * 3,
+            scratch_shapes=[dma((3,))],
+            compiler_params=pltpu.CompilerParams(vmem_limit_bytes=2**20),
+        )(*results)
+    )
 
 
 def solution(mesh):

time: 215 us -> 190 us (0.88)
  local copies, waits for them, and re-layouts: 39.7 us -> 2.53 us
  Pallas kernels: 173 us -> 187 us
    unnamed x25 -> x0, local copies, waits for them, and re-layouts: 38.3 us -> none
    pallas_call x0 -> x1, Pallas kernels: none -> 13.8 us  [gathered_by_kernel(): pl.pallas_call(settle, out_shape=[jax.ShapeDtypeStruct((8 * rows, columns...]
where the time goes in v2:
time: 190 us
  Pallas kernels  187 us (98%)
  local copies, waits for them, and re-layouts  2.53 us (1%)
    pallas_call x1, Pallas kernels, gathered_by_kernel(): pl.pallas_call(functools.partial(kernel, chunks), out_shape=[pltpu.VMEM((...  173 us
    pallas_call x1, Pallas kernels, gathered_by_kernel(): pl.pallas_call(settle, out_shape=[jax.ShapeDtypeStruct((8 * rows, columns...  13.8 us

profile of v2, /device:TPU:0, one launch (start us, length us, event | category | flops | bytes accessed | tf_op | source)
XLA Modules:
  0.0 190.0 jit_solution(10207923078518378821)
XLA Ops:
  0.6 1.3 broadcast_in_dim.6.share
  1.9 1.3 broadcast_in_dim.7.gain
  3.2 173.0 %shard_map.127 = (f32[3,1,1280]{2,1,0:T(1,128)S(1)}, bf16[3,5120,1280]{2,1,0:T(8,128)(2,1)S(1)}) custom-call(f32[1,640]{1,0:T(1,128)} %broadcast_in_dim.6.share, f32[1,640]{1,0:T(1,128)} %broadcast_in_dim.7.gain, f32[640,1280]{1,0:T(8,128)} %refs_0_.1, f32[640,1280]{1,0:T(8,128)} %refs_1_.1, f32[640,1280]{1,0:T(8,128)} %refs_2_.1, f32[640,1280]{1,0:T(8,128)} %refs_3_.1, ...), custom_call_target="tpu_custom_call" | custom-call | tf_op jit(solution)/shard_map/pallas_call | solution.py:199
  176.1 13.8 %shard_map.128 = (bf16[5120,1280]{1,0:T(8,128)(2,1)}, bf16[5120,1280]{1,0:T(8,128)(2,1)}, bf16[5120,1280]{1,0:T(8,128)(2,1)}, f32[1280]{0:T(1024)}, f32[1280]{0:T(1024)}, /*index=5*/f32[1280]{0:T(1024)}) custom-call(f32[3,1,1280]{2,1,0:T(1,128)S(1)} %get-tuple-element.8.factors, bf16[3,5120,1280]{2,1,0:T(8,128)(2,1)S(1)} %get-tuple-element.9.gathered), custom_call_target="tpu_custom_call" | custom-call | tf_op jit(solution)/shard_map/pallas_call | solution.py:227

commit v3 on v2

--- a/solution.py
+++ b/solution.py
@@ -54,8 +54,8 @@
         pl.semaphore_signal(barrier, inc=1, device_id={"rows": peer(d)}, device_id_type=MESH)
 
     for j in range(rows // LANES):
-        s = jnp.broadcast_to(share[:, j * LANES:(j + 1) * LANES], (LANES, LANES)).T
-        g = jnp.broadcast_to(gain[:, j * LANES:(j + 1) * LANES], (LANES, LANES)).T
+        s = jnp.broadcast_to(share[j * LANES:(j + 1) * LANES][None], (LANES, LANES)).T
+        g = jnp.broadcast_to(gain[j * LANES:(j + 1) * LANES][None], (LANES, LANES)).T
         wide_one[j * LANES:(j + 1) * LANES, :] = s * g
         wide_other[j * LANES:(j + 1) * LANES, :] = (1.0 - s) * g
 
@@ -181,7 +181,17 @@
 
 def settle(factors, gathered, *refs):
     targets, sems = refs[:6], refs[6]
-    copies = [pltpu.make_async_copy(gathered.at[m], targets[m], sems.at[m]) for m in range(3)]
+    parts = sems.shape[1]
+    height = gathered.shape[1] // parts
+    copies = [
+        pltpu.make_async_copy(
+            gathered.at[m, pl.ds(p * height, height), :],
+            targets[m].at[pl.ds(p * height, height), :],
+            sems.at[m, p],
+        )
+        for p in range(parts)
+        for m in range(3)
+    ]
     for c in copies:
         c.start()
     for m in range(3):
@@ -221,7 +231,7 @@
         compiler_params=pltpu.CompilerParams(
             collective_id=0, has_side_effects=True, vmem_limit_bytes=22 * 2**20
         ),
-    )(mix_share[None], norm_gain[None], *weights)
+    )(mix_share, norm_gain, *weights)
     results = [pltpu.with_memory_space_constraint(r, pltpu.VMEM) for r in results]
     return tuple(
         pl.pallas_call(
@@ -230,7 +240,7 @@
             + [jax.ShapeDtypeStruct((columns,), jnp.float32)] * 3,
             in_specs=[vmem] * 2,
             out_specs=[pl.BlockSpec(memory_space=pl.ANY)] * 3 + [vmem] * 3,
-            scratch_shapes=[dma((3,))],
+            scratch_shapes=[dma((3, 8))],
             compiler_params=pltpu.CompilerParams(vmem_limit_bytes=2**20),
         )(*results)
     )

time: 190 us -> 187 us (0.984)
  local copies, waits for them, and re-layouts: 2.53 us -> 0 us
    broadcast_in_dim x2 -> x0, local copies, waits for them, and re-layouts: 2.53 us -> none  [the longest x1 1.27 us: gathered_by_kernel(): mix_share[None]]
where the time goes in v3:
time: 187 us
  Pallas kernels  186 us (99%)
    pallas_call x1, Pallas kernels, gathered_by_kernel(): pl.pallas_call(functools.partial(kernel, chunks), out_shape=[pltpu.VMEM((...  173 us
    pallas_call x1, Pallas kernels, gathered_by_kernel(): pl.pallas_call(settle, out_shape=[jax.ShapeDtypeStruct((8 * rows, columns...  13.5 us

profile of v3, /device:TPU:0, one launch (start us, length us, event | category | flops | bytes accessed | tf_op | source)
XLA Modules:
  0.0 187.1 jit_solution(3878740668518140970)
XLA Ops:
  0.6 173.0 %shard_map.127 = (f32[3,1,1280]{2,1,0:T(1,128)S(1)}, bf16[3,5120,1280]{2,1,0:T(8,128)(2,1)S(1)}) custom-call(f32[640]{0:T(1024)} %share.1, f32[640]{0:T(1024)} %gain.1, f32[640,1280]{1,0:T(8,128)} %refs_0_.1, f32[640,1280]{1,0:T(8,128)} %refs_1_.1, f32[640,1280]{1,0:T(8,128)} %refs_2_.1, f32[640,1280]{1,0:T(8,128)} %refs_3_.1, f32[640,1280]{1,0:T(8,128)} %refs_4_.1, ...), custom_call_target="tpu_custom_call" | custom-call | tf_op jit(solution)/shard_map/pallas_call | solution.py:209
  173.6 13.5 %shard_map.128 = (bf16[5120,1280]{1,0:T(8,128)(2,1)}, bf16[5120,1280]{1,0:T(8,128)(2,1)}, bf16[5120,1280]{1,0:T(8,128)(2,1)}, f32[1280]{0:T(1024)}, f32[1280]{0:T(1024)}, /*index=5*/f32[1280]{0:T(1024)}) custom-call(f32[3,1,1280]{2,1,0:T(1,128)S(1)} %get-tuple-element.8.factors, bf16[3,5120,1280]{2,1,0:T(8,128)(2,1)S(1)} %get-tuple-element.9.gathered), custom_call_target="tpu_custom_call" | custom-call | tf_op jit(solution)/shard_map/pallas_call | solution.py:237
